TPU v7x, 32 devices: a whole 2x2x4 slice. The times are simulated.
32 devices in a mesh: subj: 4 (over y, core), vox: 8 (over z, x).
Axes of the slice: x: 2, y: 2, z: 4, core: 2. Of those that a mesh axis runs over, the one named last changes fastest.
Arguments:
- series: bfloat16 [16, 256, 16384], P('subj', None, 'vox'), may hold values from -6 to 6
- offsets: int32 [16, 12], replicated, may hold values from 0 to 240
- selected: int32 [16], replicated, may hold values from 0 to 16383, as said below
Outputs:
- kernel: float32 [16, 192, 192], P('vox', 'subj')
Inputs may be any that keep to these rules, and one draw needn't show every extreme that they name: `offsets`: each epoch lies inside its subject's run; epochs may intersect. `selected`: the ids are distinct.
All inputs are finite; a program needn't handle non-finite values.
Results may differ from a plain program's by a relative error of at most 0.00035.
Values may be sent and summed in bfloat16 or wider, within the bound.
A program may use at most 128 MiB of HBM per device.

v0:
```python
import functools

import jax
import jax.numpy as jnp
from jax import lax
from jax.experimental import pallas as pl
from jax.experimental.pallas import tpu as pltpu
from jax.sharding import PartitionSpec as P

TR = 16
KB = 8
series_floor = 1.0
spread_floor = 0.05
shrink_factor = 0.9
f32 = jnp.float32
bf16 = jnp.bfloat16


def iota(shape, dim):
    return lax.broadcasted_iota(jnp.int32, shape, dim)


def kernel(
    G, V, NS, EP, SEL, W,
    off_ref, sel_ref, series_ref, out_ref,
    ep, inv, part, slots, a_hi, a_lo, perm, send, recv, gram, rsbuf,
    slab_send, slab_recv, sc_send, sc_recv, rs_send, rs_recv,
):
    subj = lax.axis_index("subj")
    vox = lax.axis_index("vox")
    RUN = series_ref.shape[1]
    VL = series_ref.shape[2]
    ROWS = EP * TR
    H = SEL // KB
    KH = KB // G
    SL = SEL // V
    NE = NS * EP
    chunks = VL // W

    barrier = pltpu.get_barrier_semaphore()
    for dj in range(G):
        for dv in range(V):
            if dj or dv:
                pl.semaphore_signal(
                    barrier, inc=1,
                    device_id=(lax.rem(subj + dj, G), lax.rem(vox + dv, V)),
                    device_id_type=pl.DeviceIdType.MESH,
                )

    for s in range(NS):
        col = iota((TR, RUN), 1)
        row = iota((TR, RUN), 0)
        tiles = [
            jnp.where(col == row + off_ref[subj * NS + s, e], 1.0, 0.0) for e in range(EP)
        ]
        hot = jnp.concatenate(tiles, axis=0).astype(bf16)

        def gather(c, carry, hot=hot, s=s):
            at = pl.ds(pl.multiple_of(c * W, W), W)
            x = jnp.dot(hot, series_ref[s, :, at], preferred_element_type=f32)
            ep[s, :, at] = x.astype(bf16)
            x3 = x.reshape(EP, TR, W)
            total = jnp.sum(x3, axis=1)
            ssq = jnp.sum(x3 * x3, axis=1) - total * total * (1.0 / TR)
            inv[s, :, at] = shrink_factor * lax.rsqrt(jnp.maximum(ssq, 0.0) + series_floor)
            return carry

        lax.fori_loop(0, chunks, gather, 0)

    ids = jnp.zeros((SEL, 1), jnp.int32)
    which = iota((SEL, 1), 0)
    for p in range(SEL):
        ids = jnp.where(which == p, sel_ref[(p % V) * SL + p // V], ids)
    picker = jnp.where(iota((SEL, VL), 1) + vox * VL == ids, 1.0, 0.0).astype(bf16)
    for s in range(NS):
        got = lax.dot_general(
            picker, ep[s], (((1,), (1,)), ((), ())), preferred_element_type=f32
        )
        part[s] = got.astype(bf16)

    pl.semaphore_wait(barrier, G * V - 1)

    def slab_copy(d, sender):
        return pltpu.make_async_remote_copy(
            src_ref=part, dst_ref=slots.at[sender],
            send_sem=slab_send.at[d], recv_sem=slab_recv.at[d],
            device_id=(subj, lax.rem(vox + d, V)),
            device_id_type=pl.DeviceIdType.MESH,
        )

    for d in range(1, V):
        slab_copy(d, vox).start()

    out_row = iota((KB * NE, KB * NE), 0)
    in_row = iota((KB * NE, KB * NE), 1)
    source = lax.rem(out_row, NE) * KB + out_row // NE
    perm[...] = jnp.where(source == in_row, 1.0, 0.0).astype(bf16)

    for d in range(1, V):
        slab_copy(d, lax.rem(vox - d + V, V)).wait_recv()

    same = iota((ROWS, ROWS), 0) // TR == iota((ROWS, ROWS), 1) // TR
    ones = jnp.where(same, 1.0, 0.0)
    pick_e = iota((EP, KB, ROWS), 2) // TR == iota((EP, KB, ROWS), 0)
    for s in range(NS):
        slab = part[s].astype(f32)
        for d in range(1, V):
            slab = slab + slots[lax.rem(vox + d, V), s].astype(f32)
        mean = jnp.dot(
            slab, ones, precision=lax.Precision.HIGHEST, preferred_element_type=f32
        ) * (1.0 / TR)
        centred = slab - mean
        ssq = jnp.dot(
            centred * centred, ones,
            precision=lax.Precision.HIGHEST, preferred_element_type=f32,
        )
        std = centred / jnp.sqrt(ssq + series_floor)
        hi = std.astype(bf16).astype(f32)
        lo = std - hi
        for h in range(H):
            for value, where in ((hi, a_hi), (lo, a_lo)):
                block = value[h * KB:(h + 1) * KB]
                spread = jnp.where(pick_e, block[None], 0.0).reshape(EP * KB, ROWS)
                where[h, s] = spread.astype(bf16)

    def score_copy(h, d, sender, at):
        return pltpu.make_async_remote_copy(
            src_ref=send.at[h, lax.rem(subj + d, G), :, :, at],
            dst_ref=recv.at[h, :, pl.ds(pl.multiple_of(sender * NE, NE), NE), at],
            send_sem=sc_send.at[h, d], recv_sem=sc_recv.at[h, d],
            device_id=(lax.rem(subj + d, G), vox),
            device_id_type=pl.DeviceIdType.MESH,
        )

    own_rows = pl.ds(pl.multiple_of(subj * NE, NE), NE)
    for h in range(H):
        def scores(c, carry, h=h):
            at = pl.ds(pl.multiple_of(c * W, W), W)
            parts = []
            for s in range(NS):
                x = ep[s, :, at]
                corr = jnp.dot(a_hi[h, s], x, preferred_element_type=f32)
                corr = corr + jnp.dot(a_lo[h, s], x, preferred_element_type=f32)
                r = corr.reshape(EP, KB, W) * inv[s, :, at][:, None, :]
                f = 0.5 * (jnp.log(1.0 + r) - jnp.log(1.0 - r))
                f = f - jnp.sum(f, axis=0, keepdims=True) * (1.0 / EP)
                var = jnp.sum(f * f, axis=0, keepdims=True) * (1.0 / EP)
                z = f * lax.rsqrt(var + spread_floor)
                parts.append(z.reshape(EP * KB, W).astype(bf16))
            z = jnp.concatenate(parts, axis=0)
            moved = jnp.dot(perm[...], z, preferred_element_type=f32)
            send[h, :, :, :, at] = moved.astype(bf16).reshape(G, KH, NE, W)
            for d in range(1, G):
                score_copy(h, d, subj, at).start()
            recv[h, :, own_rows, at] = send[h, subj, :, :, at]
            return carry

        lax.fori_loop(0, chunks, scores, 0)

    whole = pl.ds(0, VL)

    def rs_copy(h, i, dj, owner, local):
        to = lax.rem(subj + dj, G)
        return pltpu.make_async_remote_copy(
            src_ref=gram.at[h, i, pl.ds(pl.multiple_of(to * NE, NE), NE)],
            dst_ref=rsbuf.at[local, vox],
            send_sem=rs_send.at[h, i, dj], recv_sem=rs_recv.at[local, vox],
            device_id=(to, owner),
            device_id_type=pl.DeviceIdType.MESH,
        )

    def spot(h, i):
        p = h * KB + subj * KH + i
        return lax.rem(p, V), p // V

    for h in range(H):
        for d in range(1, G):
            score_copy(h, d, lax.rem(subj - d + G, G), whole).wait_recv()
        for i in range(KH):
            rows = recv[h, i]
            gram[h, i] = lax.dot_general(
                rows, rows, (((1,), (1,)), ((), ())), preferred_element_type=f32
            )
            owner, local = spot(h, i)
            for dj in range(G):
                if dj:
                    rs_copy(h, i, dj, owner, local).start()
                else:
                    @pl.when(owner != vox)
                    def _():
                        rs_copy(h, i, 0, owner, local).start()

                    @pl.when(owner == vox)
                    def _():
                        rsbuf[local, vox] = gram[h, i, own_rows]

    for local in range(SL):
        p = local * V + vox
        handler = lax.rem(p, KB) // KH
        total = None
        for v in range(V):
            @pl.when(jnp.logical_or(handler != subj, vox != v))
            def _():
                pltpu.make_async_remote_copy(
                    src_ref=gram.at[0, 0, pl.ds(0, NE)],
                    dst_ref=rsbuf.at[local, v],
                    send_sem=rs_send.at[0, 0, 0], recv_sem=rs_recv.at[local, v],
                    device_id=(subj, lax.rem(vox + 1, V)),
                    device_id_type=pl.DeviceIdType.MESH,
                ).wait_recv()
            term = rsbuf[local, v]
            total = term if total is None else total + term
        out_ref[local] = total * (1.0 / (VL * V))

    for d in range(1, V):
        slab_copy(d, vox).wait_send()
    for h in range(H):
        for d in range(1, G):
            score_copy(h, d, subj, whole).wait_send()
        for i in range(KH):
            owner, local = spot(h, i)
            for dj in range(G):
                if dj:
                    rs_copy(h, i, dj, owner, local).wait_send()
                else:
                    @pl.when(owner != vox)
                    def _():
                        rs_copy(h, i, 0, owner, local).wait_send()


def body(series, offsets, selected):
    G = lax.axis_size("subj")
    V = lax.axis_size("vox")
    NS, RUN, VL = series.shape
    EP = offsets.shape[1]
    SEL = selected.shape[0]
    W = 256
    NE = NS * EP
    ROWS = EP * TR
    H = SEL // KB
    KH = KB // G
    SL = SEL // V
    vm = pltpu.VMEM
    dma = pltpu.SemaphoreType.DMA
    return pl.pallas_call(
        functools.partial(kernel, G, V, NS, EP, SEL, W),
        out_shape=jax.ShapeDtypeStruct((SL, NE, G * NE), f32),
        in_specs=[
            pl.BlockSpec(memory_space=pltpu.SMEM),
            pl.BlockSpec(memory_space=pltpu.SMEM),
            pl.BlockSpec(memory_space=pltpu.VMEM),
        ],
        out_specs=pl.BlockSpec(memory_space=pltpu.VMEM),
        scratch_shapes=[
            vm((NS, ROWS, VL), bf16),
            vm((NS, EP, VL), f32),
            vm((NS, SEL, ROWS), bf16),
            vm((V, NS, SEL, ROWS), bf16),
            vm((H, NS, EP * KB, ROWS), bf16),
            vm((H, NS, EP * KB, ROWS), bf16),
            vm((KB * NE, KB * NE), bf16),
            vm((H, G, KH, NE, VL), bf16),
            vm((H, KH, G * NE, VL), bf16),
            vm((H, KH, G * NE, G * NE), f32),
            vm((SL, V, NE, G * NE), f32),
            dma((V,)),
            dma((V,)),
            dma((H, G)),
            dma((H, G)),
            dma((H, KH, G)),
            dma((SL, V)),
        ],
        compiler_params=pltpu.CompilerParams(
            collective_id=0, has_side_effects=True, vmem_limit_bytes=56 * 1024 * 1024
        ),
    )(offsets, selected, series)


def solution(mesh):
    placed = (P("subj", None, "vox"), P(), P())
    return jax.shard_map(
        body, mesh=mesh, in_specs=placed, out_specs=P("vox", "subj", None), check_vma=False
    )
```

profile of v0, /device:TPU:7, one launch (start us, length us, event | category | flops | bytes accessed | tf_op | source)
XLA Modules:
  0.0 90.4 jit_solution(9216068207952142671)
XLA Ops:
  0.0 88.8 %shard_map.37 = f32[2,48,192]{2,1,0:T(8,128)} custom-call(s32[16,12]{1,0:T(8,128)} %off_ref.1, s32[16]{0:T(128)} %sel_ref.1, bf16[4,256,2048]{2,1,0:T(8,128)(2,1)} %series_ref.1), custom_call_target="tpu_custom_call" | custom-call | tf_op jit(solution)/shard_map/pallas_call | solution.py:245
  88.8 1.5 %copy.5 = f32[2,48,192]{2,1,0:T(8,128)} copy(f32[2,48,192]{2,1,0:T(8,128)} %shard_map.37) | data formatting | bytes 147456
where the time goes:
time: 90.6 us; the launch traced here: 90.4 us
  Pallas kernels  88.8 us (98%)
  local copies, waits for them, and re-layouts  1.54 us (2%)
    pallas_call x1, Pallas kernels, body(): pl.pallas_call(functools.partial(kernel, G, V, NS, EP, SEL, W), out_shape...  88.8 us

commit v1 on v0

v1 whole, which is shorter than its diff:
```python
import functools

import jax
import jax.numpy as jnp
from jax import lax
from jax.experimental import pallas as pl
from jax.experimental.pallas import tpu as pltpu
from jax.sharding import PartitionSpec as P

TR = 16
KB = 8
series_floor = 1.0
spread_floor = 0.05
shrink_factor = 0.9
f32 = jnp.float32
bf16 = jnp.bfloat16


def iota(shape, dim):
    return lax.broadcasted_iota(jnp.int32, shape, dim)


def pieces_of(G, V, NE):
    R = V
    while R > G and (V % R or R % G or (G * NE) % R or (G * NE // R) % 8):
        R -= 1
    return R


def kernel(
    G, V, NS, EP, SEL, W,
    off_ref, sel_ref, series_ref, out_ref,
    ep, hot, inv, part, slots, a_hi, a_lo, perm, send, recv,
    gram, pieces_in, summed, landed,
    slab_send, slab_recv, sc_send, sc_recv, rs_send, rs_recv, fin_send, fin_recv,
):
    subj = lax.axis_index("subj")
    vox = lax.axis_index("vox")
    RUN = series_ref.shape[1]
    VL = series_ref.shape[2]
    ROWS = EP * TR
    H = SEL // KB
    KH = KB // G
    SL = SEL // V
    NE = NS * EP
    chunks = VL // W
    R = pieces_of(G, V, NE)
    VR = V // R
    RP = G * NE // R
    PG = R // G
    ORDER = tuple(range(G // 2, G)) + tuple(range(1, G // 2))

    barrier = pltpu.get_barrier_semaphore()
    for dj in range(G):
        for dv in range(V):
            if dj or dv:
                pl.semaphore_signal(
                    barrier, inc=1,
                    device_id=(lax.rem(subj + dj, G), lax.rem(vox + dv, V)),
                    device_id_type=pl.DeviceIdType.MESH,
                )

    ids = jnp.zeros((SEL, 1), jnp.int32)
    which = iota((SEL, 1), 0)
    for p in range(SEL):
        ids = jnp.where(which == p, sel_ref[(p % V) * SL + p // V], ids)
    picker = jnp.where(iota((SEL, VL), 1) + vox * VL == ids, 1.0, 0.0).astype(bf16)
    col = iota((TR, RUN), 1) - iota((TR, RUN), 0)
    pieces = []
    for s in range(NS):
        tiles = [
            jnp.where(col == off_ref[subj * NS + s, e], 1.0, 0.0) for e in range(EP)
        ]
        hot[s] = jnp.concatenate(tiles, axis=0).astype(bf16)
        runs = lax.dot_general(
            picker, series_ref[s], (((1,), (1,)), ((), ())), preferred_element_type=f32
        )
        pieces.append(lax.dot_general(
            runs.astype(bf16), hot[s], (((1,), (1,)), ((), ())), preferred_element_type=f32
        ))
    joined = jnp.concatenate(pieces, axis=1)
    for h in range(H):
        part[h] = joined[h * KB:(h + 1) * KB].astype(bf16)

    pl.semaphore_wait(barrier, G * V - 1)

    def slab_copy(h, d, sender):
        return pltpu.make_async_remote_copy(
            src_ref=part.at[h], dst_ref=slots.at[h, sender],
            send_sem=slab_send.at[h, d], recv_sem=slab_recv.at[h, d],
            device_id=(subj, lax.rem(vox + d, V)),
            device_id_type=pl.DeviceIdType.MESH,
        )

    for h in range(H):
        for d in range(1, V):
            slab_copy(h, d, vox).start()

    def gather(c, carry):
        at = pl.ds(pl.multiple_of(c * W, W), W)
        for s in range(NS):
            x = jnp.dot(hot[s], series_ref[s, :, at], preferred_element_type=f32)
            ep[s, :, at] = x.astype(bf16)
            x3 = x.reshape(EP, TR, W)
            total = jnp.sum(x3, axis=1)
            ssq = jnp.sum(x3 * x3, axis=1) - total * total * (1.0 / TR)
            inv[s, :, at] = shrink_factor * lax.rsqrt(jnp.maximum(ssq, 0.0) + series_floor)
        return carry

    lax.fori_loop(0, chunks, gather, 0)

    out_row = iota((KB * NE, KB * NE), 0)
    in_row = iota((KB * NE, KB * NE), 1)
    slot = out_row // NE
    source = lax.rem(out_row, NE) * KB + lax.rem(slot, KH) * G + slot // KH
    perm[...] = jnp.where(source == in_row, 1.0, 0.0).astype(bf16)

    same = iota((ROWS, ROWS), 0) // TR == iota((ROWS, ROWS), 1) // TR
    ones = jnp.where(same, 1.0, 0.0)
    pick_e = iota((EP, KB, ROWS), 2) // TR == iota((EP, KB, ROWS), 0)

    def slab_rows(h):
        slab = part[h].astype(f32)
        for d in range(1, V):
            slab_copy(h, d, lax.rem(vox - d + V, V)).wait_recv()
        for d in range(1, V):
            slab = slab + slots[h, lax.rem(vox + d, V)].astype(f32)
        rows = jnp.concatenate(
            [slab[:, s * ROWS:(s + 1) * ROWS] for s in range(NS)], axis=0
        )
        mean = jnp.dot(
            rows.astype(bf16), ones.astype(bf16), preferred_element_type=f32
        ) * (1.0 / TR)
        centred = rows - mean
        ssq = jnp.dot(
            centred * centred, ones,
            precision=lax.Precision.HIGHEST, preferred_element_type=f32,
        )
        std = centred / jnp.sqrt(ssq + series_floor)
        hi = std.astype(bf16).astype(f32)
        lo = std - hi
        for s in range(NS):
            for value, where in ((hi, a_hi), (lo, a_lo)):
                block = value[s * KB:(s + 1) * KB]
                spread = jnp.where(pick_e, block[None], 0.0).reshape(EP * KB, ROWS)
                where[h, s] = spread.astype(bf16)

    every = pl.ds(0, VL)

    def score_copy(h, i, n, d, sender, at):
        return pltpu.make_async_remote_copy(
            src_ref=send.at[h, lax.rem(subj + d, G), pl.ds(i, n), :, at],
            dst_ref=recv.at[h, pl.ds(i, n), pl.ds(pl.multiple_of(sender * NE, NE), NE), at],
            send_sem=sc_send.at[h, i, d], recv_sem=sc_recv.at[h, i, d],
            device_id=(lax.rem(subj + d, G), vox),
            device_id_type=pl.DeviceIdType.MESH,
        )

    def groups(h):
        return ((0, KH),) if h == 0 else tuple((i, 1) for i in range(KH))

    own_rows = pl.ds(pl.multiple_of(subj * NE, NE), NE)
    for h in range(H):
        slab_rows(h)

        def scores(c, carry, h=h):
            at = pl.ds(pl.multiple_of(c * W, W), W)
            parts = []
            for s in range(NS):
                x = ep[s, :, at]
                corr = jnp.dot(a_hi[h, s], x, preferred_element_type=f32)
                corr = corr + jnp.dot(a_lo[h, s], x, preferred_element_type=f32)
                r = corr.reshape(EP, KB, W) * inv[s, :, at][:, None, :]
                f = 0.5 * (jnp.log(1.0 + r) - jnp.log(1.0 - r))
                f = f - jnp.sum(f, axis=0, keepdims=True) * (1.0 / EP)
                var = jnp.sum(f * f, axis=0, keepdims=True) * (1.0 / EP)
                z = f * lax.rsqrt(var + spread_floor)
                parts.append(z.reshape(EP * KB, W).astype(bf16))
            z = jnp.concatenate(parts, axis=0)
            moved = jnp.dot(perm[...], z, preferred_element_type=f32)
            send[h, :, :, :, at] = moved.astype(bf16).reshape(G, KH, NE, W)
            if h == 0:
                for d in ORDER:
                    score_copy(h, 0, KH, d, subj, at).start()
            recv[h, :, own_rows, at] = send[h, subj, :, :, at]
            return carry

        lax.fori_loop(0, chunks, scores, 0)

        if h:
            for i, n in groups(h):
                for d in ORDER:
                    score_copy(h, i, n, d, subj, every).start()

    def row_piece(r):
        return pl.ds(pl.multiple_of(r * RP, RP), RP)

    def part_copy(t, d):
        to = lax.rem(vox + d, V)
        return pltpu.make_async_remote_copy(
            src_ref=gram.at[t, row_piece(to // VR)], dst_ref=pieces_in.at[t, d - 1],
            send_sem=rs_send.at[t, d], recv_sem=rs_recv.at[t],
            device_id=(subj, to), device_id_type=pl.DeviceIdType.MESH,
        )

    def all_parts(t):
        return pltpu.make_async_remote_copy(
            src_ref=pieces_in.at[t], dst_ref=pieces_in.at[t],
            send_sem=rs_send.at[t, 0], recv_sem=rs_recv.at[t],
            device_id=(subj, lax.rem(vox + 1, V)), device_id_type=pl.DeviceIdType.MESH,
        )

    piece = vox // VR
    to_subj = piece // PG
    to_rows = lax.rem(piece, PG)

    def reduces(v):
        return lax.rem(v, VR) == 0

    def spot(t):
        p = t * G + subj
        return lax.rem(p, V), p // V

    def final_copy(t):
        owner, local = spot(t)
        return pltpu.make_async_remote_copy(
            src_ref=summed.at[t], dst_ref=landed.at[local, to_rows],
            send_sem=fin_send.at[t], recv_sem=fin_recv.at[local, to_rows],
            device_id=(to_subj, owner), device_id_type=pl.DeviceIdType.MESH,
        )

    def away(t):
        owner, local = spot(t)
        return jnp.logical_or(to_subj != subj, owner != vox)

    def finish(t):
        @pl.when(reduces(vox))
        def _():
            all_parts(t).wait_recv()
            total = gram[t, row_piece(piece)]
            for d in range(1, V):
                total = total + pieces_in[t, d - 1]
            total = total * (1.0 / (VL * V))
            summed[t] = total

            @pl.when(away(t))
            def _():
                final_copy(t).start()

            @pl.when(jnp.logical_not(away(t)))
            def _():
                landed[spot(t)[1], to_rows] = total

    T = H * KH
    for h in range(H):
        for i in range(KH):
            t = h * KH + i
            for first, n in groups(h):
                if first == i:
                    for d in range(1, G):
                        sender = lax.rem(subj - d + G, G)
                        score_copy(h, i, n, d, sender, every).wait_recv()
            rows = recv[h, i]
            gram[t] = lax.dot_general(
                rows, rows, (((1,), (1,)), ((), ())), preferred_element_type=f32
            )
            for d in range(1, V):
                @pl.when(reduces(lax.rem(vox + d, V)))
                def _():
                    part_copy(t, d).start()
            if t:
                finish(t - 1)
    finish(T - 1)

    for local in range(SL):
        p = local * V + vox
        handler = lax.rem(p, G)
        for b in range(PG):
            source = (subj * PG + b) * VR

            @pl.when(jnp.logical_or(handler != subj, source != vox))
            def _():
                pltpu.make_async_remote_copy(
                    src_ref=summed.at[0], dst_ref=landed.at[local, b],
                    send_sem=fin_send.at[0], recv_sem=fin_recv.at[local, b],
                    device_id=(subj, lax.rem(vox + 1, V)),
                    device_id_type=pl.DeviceIdType.MESH,
                ).wait_recv()
            out_ref[local, b * RP:(b + 1) * RP] = landed[local, b]

    for h in range(H):
        for d in range(1, V):
            slab_copy(h, d, vox).wait_send()
        for i, n in groups(h):
            for d in range(1, G):
                score_copy(h, i, n, d, subj, every).wait_send()
    for t in range(T):
        for d in range(1, V):
            @pl.when(reduces(lax.rem(vox + d, V)))
            def _():
                part_copy(t, d).wait_send()

        @pl.when(jnp.logical_and(reduces(vox), away(t)))
        def _():
            final_copy(t).wait_send()


def body(series, offsets, selected):
    G = lax.axis_size("subj")
    V = lax.axis_size("vox")
    NS, RUN, VL = series.shape
    EP = offsets.shape[1]
    SEL = selected.shape[0]
    W = 256
    NE = NS * EP
    ROWS = EP * TR
    H = SEL // KB
    KH = KB // G
    SL = SEL // V
    R = pieces_of(G, V, NE)
    RP = G * NE // R
    vm = pltpu.VMEM
    dma = pltpu.SemaphoreType.DMA
    return pl.pallas_call(
        functools.partial(kernel, G, V, NS, EP, SEL, W),
        out_shape=jax.ShapeDtypeStruct((SL, NE, G * NE), f32),
        in_specs=[
            pl.BlockSpec(memory_space=pltpu.SMEM),
            pl.BlockSpec(memory_space=pltpu.SMEM),
            pl.BlockSpec(memory_space=pltpu.VMEM),
        ],
        out_specs=pl.BlockSpec(memory_space=pltpu.VMEM),
        scratch_shapes=[
            vm((NS, ROWS, VL), bf16),
            vm((NS, ROWS, RUN), bf16),
            vm((NS, EP, VL), f32),
            vm((H, KB, NS * ROWS), bf16),
            vm((H, V, KB, NS * ROWS), bf16),
            vm((H, NS, EP * KB, ROWS), bf16),
            vm((H, NS, EP * KB, ROWS), bf16),
            vm((KB * NE, KB * NE), bf16),
            vm((H, G, KH, NE, VL), bf16),
            vm((H, KH, G * NE, VL), bf16),
            vm((H * KH, G * NE, G * NE), f32),
            vm((H * KH, V - 1, RP, G * NE), f32),
            vm((H * KH, RP, G * NE), f32),
            vm((SL, R // G, RP, G * NE), f32),
            dma((H, V)),
            dma((H, V)),
            dma((H, KH, G)),
            dma((H, KH, G)),
            dma((H * KH, V)),
            dma((H * KH,)),
            dma((H * KH,)),
            dma((SL, R // G)),
        ],
        compiler_params=pltpu.CompilerParams(
            collective_id=0, has_side_effects=True, vmem_limit_bytes=56 * 1024 * 1024
        ),
    )(offsets, selected, series)


def solution(mesh):
    placed = (P("subj", None, "vox"), P(), P())
    return jax.shard_map(
        body, mesh=mesh, in_specs=placed, out_specs=P("vox", "subj", None), check_vma=False
    )
```

time: 90.6 us -> 61.4 us (0.68)
  the two profiles are of different devices: /device:TPU:7 before, /device:TPU:25 now
where the time goes in v1:
time: 61.4 us; the launch traced here: 61.2 us
  Pallas kernels  59.6 us (97%)
  local copies, waits for them, and re-layouts  1.54 us (3%)
    pallas_call x1, Pallas kernels, body(): pl.pallas_call(functools.partial(kernel, G, V, NS, EP, SEL, W), out_shape...  59.6 us
    unnamed x1, local copies, waits for them, and re-layouts  1.54 us

profile of v1, /device:TPU:25, one launch (start us, length us, event | category | flops | bytes accessed | tf_op | source)
XLA Modules:
  0.0 61.2 jit_solution(8504974994577390579)
XLA Ops:
  0.0 59.6 %shard_map.37 = f32[2,48,192]{2,1,0:T(8,128)} custom-call(s32[16,12]{1,0:T(8,128)} %off_ref.1, s32[16]{0:T(128)} %sel_ref.1, bf16[4,256,2048]{2,1,0:T(8,128)(2,1)} %series_ref.1), custom_call_target="tpu_custom_call" | custom-call | tf_op jit(solution)/shard_map/pallas_call | solution.py:324
  59.6 1.5 %copy.5 = f32[2,48,192]{2,1,0:T(8,128)} copy(f32[2,48,192]{2,1,0:T(8,128)} %shard_map.37) | data formatting | bytes 147456

commit v2 on v1

--- a/solution.py
+++ b/solution.py
@@ -29,8 +29,8 @@
 
 def kernel(
     G, V, NS, EP, SEL, W,
-    off_ref, sel_ref, series_ref, out_ref,
-    ep, hot, inv, part, slots, a_hi, a_lo, perm, send, recv,
+    off_ref, sel_ref, series_hbm, out_ref,
+    series_ref, load_sem, ep, hot, inv, part, slots, a_hi, a_lo, perm, send, recv,
     gram, pieces_in, summed, landed,
     slab_send, slab_recv, sc_send, sc_recv, rs_send, rs_recv, fin_send, fin_recv,
 ):
@@ -51,14 +51,22 @@
     ORDER = tuple(range(G // 2, G)) + tuple(range(1, G // 2))
 
     barrier = pltpu.get_barrier_semaphore()
-    for dj in range(G):
-        for dv in range(V):
-            if dj or dv:
-                pl.semaphore_signal(
-                    barrier, inc=1,
-                    device_id=(lax.rem(subj + dj, G), lax.rem(vox + dv, V)),
-                    device_id_type=pl.DeviceIdType.MESH,
-                )
+    for d in range(1, G):
+        pl.semaphore_signal(
+            barrier, inc=1, device_id=(lax.rem(subj + d, G), vox),
+            device_id_type=pl.DeviceIdType.MESH,
+        )
+    for d in range(1, V):
+        pl.semaphore_signal(
+            barrier, inc=1, device_id=(subj, lax.rem(vox + d, V)),
+            device_id_type=pl.DeviceIdType.MESH,
+        )
+
+    def load(s):
+        return pltpu.make_async_copy(series_hbm.at[s], series_ref.at[s], load_sem.at[s])
+
+    for s in range(NS):
+        load(s).start()
 
     ids = jnp.zeros((SEL, 1), jnp.int32)
     which = iota((SEL, 1), 0)
@@ -72,6 +80,7 @@
             jnp.where(col == off_ref[subj * NS + s, e], 1.0, 0.0) for e in range(EP)
         ]
         hot[s] = jnp.concatenate(tiles, axis=0).astype(bf16)
+        load(s).wait()
         runs = lax.dot_general(
             picker, series_ref[s], (((1,), (1,)), ((), ())), preferred_element_type=f32
         )
@@ -82,7 +91,7 @@
     for h in range(H):
         part[h] = joined[h * KB:(h + 1) * KB].astype(bf16)
 
-    pl.semaphore_wait(barrier, G * V - 1)
+    pl.semaphore_wait(barrier, G + V - 2)
 
     def slab_copy(h, d, sender):
         return pltpu.make_async_remote_copy(
@@ -327,10 +336,12 @@
         in_specs=[
             pl.BlockSpec(memory_space=pltpu.SMEM),
             pl.BlockSpec(memory_space=pltpu.SMEM),
-            pl.BlockSpec(memory_space=pltpu.VMEM),
+            pl.BlockSpec(memory_space=pl.ANY),
         ],
         out_specs=pl.BlockSpec(memory_space=pltpu.VMEM),
         scratch_shapes=[
+            vm((NS, RUN, VL), bf16),
+            dma((NS,)),
             vm((NS, ROWS, VL), bf16),
             vm((NS, ROWS, RUN), bf16),
             vm((NS, EP, VL), f32),

time: 61.4 us -> 60.1 us (0.979)
  Pallas kernels: 59.6 us -> 57.8 us
    pallas_call x1, Pallas kernels: 59.6 us -> 57.8 us  [body(): pl.pallas_call(functools.partial(kernel, G, V, NS, EP, SEL, W), out_shape...]
where the time goes in v2:
time: 60.1 us; the launch traced here: 59.3 us
  Pallas kernels  57.8 us (96%)
  local copies, waits for them, and re-layouts  1.54 us (3%)
    pallas_call x1, Pallas kernels, body(): pl.pallas_call(functools.partial(kernel, G, V, NS, EP, SEL, W), out_shape...  57.8 us
    unnamed x1, local copies, waits for them, and re-layouts  1.54 us

profile of v2, /device:TPU:25, one launch (start us, length us, event | category | flops | bytes accessed | tf_op | source)
XLA Modules:
  0.0 59.3 jit_solution(12116438194648837494)
XLA Ops:
  0.0 57.8 %shard_map.37 = f32[2,48,192]{2,1,0:T(8,128)} custom-call(s32[16,12]{1,0:T(8,128)} %off_ref.1, s32[16]{0:T(128)} %sel_ref.1, bf16[4,256,2048]{2,1,0:T(8,128)(2,1)} %series_hbm.1), custom_call_target="tpu_custom_call" | custom-call | tf_op jit(solution)/shard_map/pallas_call | solution.py:333
  57.8 1.5 %copy.5 = f32[2,48,192]{2,1,0:T(8,128)} copy(f32[2,48,192]{2,1,0:T(8,128)} %shard_map.37) | data formatting | bytes 147456

commit v3 on v2

--- a/solution.py
+++ b/solution.py
@@ -9,6 +9,7 @@
 
 TR = 16
 KB = 8
+C1 = 4
 series_floor = 1.0
 spread_floor = 0.05
 shrink_factor = 0.9
@@ -80,6 +81,7 @@
             jnp.where(col == off_ref[subj * NS + s, e], 1.0, 0.0) for e in range(EP)
         ]
         hot[s] = jnp.concatenate(tiles, axis=0).astype(bf16)
+    for s in range(NS):
         load(s).wait()
         runs = lax.dot_general(
             picker, series_ref[s], (((1,), (1,)), ((), ())), preferred_element_type=f32
@@ -90,20 +92,6 @@
     joined = jnp.concatenate(pieces, axis=1)
     for h in range(H):
         part[h] = joined[h * KB:(h + 1) * KB].astype(bf16)
-
-    pl.semaphore_wait(barrier, G + V - 2)
-
-    def slab_copy(h, d, sender):
-        return pltpu.make_async_remote_copy(
-            src_ref=part.at[h], dst_ref=slots.at[h, sender],
-            send_sem=slab_send.at[h, d], recv_sem=slab_recv.at[h, d],
-            device_id=(subj, lax.rem(vox + d, V)),
-            device_id_type=pl.DeviceIdType.MESH,
-        )
-
-    for h in range(H):
-        for d in range(1, V):
-            slab_copy(h, d, vox).start()
 
     def gather(c, carry):
         at = pl.ds(pl.multiple_of(c * W, W), W)
@@ -116,13 +104,28 @@
             inv[s, :, at] = shrink_factor * lax.rsqrt(jnp.maximum(ssq, 0.0) + series_floor)
         return carry
 
-    lax.fori_loop(0, chunks, gather, 0)
+    after = chunks * C1 // 8
+    pl.semaphore_wait(barrier, G + V - 2)
+
+    def slab_copy(h, d, sender):
+        return pltpu.make_async_remote_copy(
+            src_ref=part.at[h], dst_ref=slots.at[h, sender],
+            send_sem=slab_send.at[h, d], recv_sem=slab_recv.at[h, d],
+            device_id=(subj, lax.rem(vox + d, V)),
+            device_id_type=pl.DeviceIdType.MESH,
+        )
+
+    for h in range(H):
+        for d in range(1, V):
+            slab_copy(h, d, vox).start()
 
     out_row = iota((KB * NE, KB * NE), 0)
     in_row = iota((KB * NE, KB * NE), 1)
     slot = out_row // NE
     source = lax.rem(out_row, NE) * KB + lax.rem(slot, KH) * G + slot // KH
     perm[...] = jnp.where(source == in_row, 1.0, 0.0).astype(bf16)
+
+    lax.fori_loop(0, after, gather, 0)
 
     same = iota((ROWS, ROWS), 0) // TR == iota((ROWS, ROWS), 1) // TR
     ones = jnp.where(same, 1.0, 0.0)
@@ -173,6 +176,11 @@
         slab_rows(h)
 
         def scores(c, carry, h=h):
+            if h == 0 and after < chunks:
+                @pl.when(c >= after)
+                def _():
+                    gather(c, 0)
+
             at = pl.ds(pl.multiple_of(c * W, W), W)
             parts = []
             for s in range(NS):

time: 60.1 us -> 59.5 us (0.990)
  no operation moved by 1% of the time
where the time goes in v3:
time: 59.5 us; the launch traced here: 58.9 us
  Pallas kernels  57.4 us (96%)
  local copies, waits for them, and re-layouts  1.54 us (3%)
    pallas_call x1, Pallas kernels, body(): pl.pallas_call(functools.partial(kernel, G, V, NS, EP, SEL, W), out_shape...  57.4 us
    unnamed x1, local copies, waits for them, and re-layouts  1.54 us

profile of v3, /device:TPU:25, one launch (start us, length us, event | category | flops | bytes accessed | tf_op | source)
XLA Modules:
  0.0 58.9 jit_solution(11215177106066046716)
XLA Ops:
  0.0 57.4 %shard_map.37 = f32[2,48,192]{2,1,0:T(8,128)} custom-call(s32[16,12]{1,0:T(8,128)} %off_ref.1, s32[16]{0:T(128)} %sel_ref.1, bf16[4,256,2048]{2,1,0:T(8,128)(2,1)} %series_hbm.1), custom_call_target="tpu_custom_call" | custom-call | tf_op jit(solution)/shard_map/pallas_call | solution.py:341
  57.4 1.5 %copy.5 = f32[2,48,192]{2,1,0:T(8,128)} copy(f32[2,48,192]{2,1,0:T(8,128)} %shard_map.37) | data formatting | bytes 147456
